TPU v7x, 32 devices: a whole 2x2x4 slice. The times are simulated.
32 devices in a mesh: owner: 4 (over x, core), rows: 8 (over z, y).
Axes of the slice: x: 2, y: 2, z: 4, core: 2. Of those that a mesh axis runs over, the one named last changes fastest.
Arguments:
- master_gate: float32 [64, 2048, 1408], P('owner', 'rows'), may hold values from -0.1875 to 0.1875
- master_up: float32 [64, 2048, 1408], P('owner', 'rows'), may hold values from -0.1875 to 0.1875
- router_weight: float32 [2048, 64], P('rows', 'owner'), may hold values from -0.125 to 0.125
- router_gain: float32 [2048], P('rows'), may hold values from 0.25 to 1.75
Outputs:
- final_gate: bfloat16 [64, 2048, 1408], P('owner', None, 'rows')
- final_up: bfloat16 [64, 2048, 1408], P('owner', None, 'rows')
- scale_gate: float32 [64, 1408], P('owner', 'rows')
- scale_up: float32 [64, 1408], P('owner', 'rows')
- serve_router: bfloat16 [2048, 64], replicated
All inputs are finite; a program needn't handle non-finite values. Where the computation divides by a largest or mean magnitude, that divisor is 1e-20 or more.
Results may differ from a plain program's by a relative error of at most 0.001.
Values may be sent and summed in bfloat16 or wider, within the bound.
A program may use at most 192 MiB of HBM per device.

v0:
```python
import functools

import jax
import jax.numpy as jnp
from jax import lax
from jax.experimental import pallas as pl
from jax.experimental.pallas import tpu as pltpu
from jax.sharding import PartitionSpec as P

MESH = pl.DeviceIdType.MESH
LANES = 128
SUBLANES = 8
PACKED = 16
SLOTS = 4
PER_SEND = 2
VMEM_FOR_BLOCKS = 48 * 1024 * 1024
VMEM_FOR_REST = 2 * 1024 * 1024


def kernel(
    owners,
    peers,
    gate,
    up,
    router,
    gain,
    out_gate,
    out_up,
    out_router,
    scales_first,
    scales_rest,
    slots,
    largest_first,
    largest_rest,
    parts_first,
    parts_rest,
    send,
    row,
    slot_sem,
    send_sem,
    recv_sem,
    part_send,
    part_recv,
    whole_send,
    whole_recv,
    router_send,
    router_recv,
):
    owner, me = lax.axis_index("owner"), lax.axis_index("rows")
    experts, rows, width = gate.shape
    tiles = width // LANES
    cut = width // peers
    masters, outs = (gate, up), (out_gate, out_up)
    largest, parts = (largest_first, largest_rest), (parts_first, parts_rest)
    scales = (scales_first, scales_rest)
    lanes = pl.ds(pl.multiple_of(me * rows, LANES), rows)

    pairs = peers & (peers - 1) == 0

    def partner(k):
        if not pairs:
            return lax.rem(me + k, peers)
        bits = [1 << b for b in range(peers.bit_length() - 1) if k >> b & 1]
        return sum((bit - 2 * bit * lax.rem(me // bit, 2) for bit in bits), me)

    def origin(k):
        return partner(k) if pairs else lax.rem(me + peers - k, peers)

    def fetch(m, first, i):
        s = lax.rem(i, SLOTS)
        return pltpu.make_async_copy(masters[m].at[first + i], slots.at[s], slot_sem.at[s])

    def begin(m, first, length):
        for i in range(min(SLOTS, length)):
            fetch(m, first, i).start()

    def advance(m, first, length, i):
        if length > SLOTS:

            @pl.when(i + SLOTS < length)
            def _():
                fetch(m, first, i + SLOTS).start()

    def place(m, e, c, first):
        k = m * experts + e - (0 if first else SUBLANES)
        return (k // SUBLANES) * tiles + c, pl.ds(lax.rem(k, SUBLANES), 1)

    def maxima(m, first, length):
        stage = 0 if m == 0 and first < SUBLANES else 1

        def body(i, _):
            fetch(m, first, i).wait()
            for c in range(tiles):
                x = slots[lax.rem(i, SLOTS), :, c * LANES : (c + 1) * LANES]
                tile, sub = place(m, first + i, c, stage == 0)
                largest[stage][tile, sub, :] = jnp.max(jnp.abs(x), axis=0, keepdims=True)
            advance(m, first, length, i)
            return 0

        lax.fori_loop(0, length, body, 0)

    def part_copy(stage, k):
        per = parts[stage].shape[1]
        to = partner(k)
        return pltpu.make_async_remote_copy(
            src_ref=largest[stage].at[pl.ds(to * per, per)],
            dst_ref=parts[stage].at[k],
            send_sem=part_send.at[stage, k],
            recv_sem=part_recv.at[stage, k],
            device_id={"rows": to},
            device_id_type=MESH,
        )

    def share(stage, of):
        per = parts[stage].shape[1]
        return scales[stage].at[pl.ds(of * per, per)]

    def whole_copy(stage, k):
        return pltpu.make_async_remote_copy(
            src_ref=share(stage, me),
            dst_ref=share(stage, me),
            send_sem=whole_send.at[stage, k],
            recv_sem=whole_recv.at[stage, k],
            device_id={"rows": partner(k)},
            device_id_type=MESH,
        )

    order = sorted(range(1, peers), key=lambda k: (k.bit_length(), k))

    def scatter(stage):
        for k in order:
            part_copy(stage, k).start()

    def reduce(stage):
        per = parts[stage].shape[1]
        total = largest[stage][pl.ds(me * per, per)]
        for k in order:
            part_copy(stage, k).wait_recv()
            total = jnp.maximum(total, parts[stage][k])
        share(stage, me)[...] = total
        for k in order:
            whole_copy(stage, k).start()

    def gathered(stage):
        for k in order:
            part_copy(stage, k).wait_send()
            there = share(stage, origin(k))
            pltpu.make_async_copy(there, there, whole_recv.at[stage, k]).wait()
            whole_copy(stage, k).wait_send()

    def send_copy(m, k, e, length):
        to = partner(k)
        return pltpu.make_async_remote_copy(
            src_ref=send.at[m, pl.ds(e, length), pl.ds(pl.multiple_of(to * cut, PACKED), cut), :],
            dst_ref=outs[m].at[pl.ds(e, length), :, lanes],
            send_sem=send_sem.at[m, k],
            recv_sem=recv_sem.at[m, k],
            device_id={"rows": to},
            device_id_type=MESH,
        )

    def keep_copy(m, e, length):
        return pltpu.make_async_copy(
            send.at[m, pl.ds(e, length), pl.ds(pl.multiple_of(me * cut, PACKED), cut), :],
            outs[m].at[pl.ds(e, length), :, lanes],
            send_sem.at[m, 0],
        )

    def bulk(m, first, length, batch):
        stage = 0 if m == 0 and first < SUBLANES else 1

        def body(step, _):
            for j in range(batch):
                i = step * batch + j
                fetch(m, first, i).wait()
                for c in range(tiles):
                    x = slots[lax.rem(i, SLOTS), :, c * LANES : (c + 1) * LANES]
                    tile, sub = place(m, first + i, c, stage == 0)
                    s = scales[stage][tile, sub, :]
                    send[m, first + i, c * LANES : (c + 1) * LANES, :] = (x / s).T.astype(send.dtype)
                advance(m, first, length, i)
            for k in order:
                send_copy(m, k, first + step * batch, batch).start()
            keep_copy(m, first + step * batch, batch).start()
            return 0

        lax.fori_loop(0, length // batch, body, 0)

    depth = router.shape[0]
    block = out_router.at[pl.ds(pl.multiple_of(owner * depth, PACKED), depth), lanes]
    flat = owner * peers + me
    count = owners * peers

    def router_copy(k):
        to = lax.rem(flat + k, count)
        return pltpu.make_async_remote_copy(
            src_ref=row,
            dst_ref=block,
            send_sem=router_send.at[k],
            recv_sem=router_recv.at[k],
            device_id={"owner": to // peers, "rows": lax.rem(to, peers)},
            device_id_type=MESH,
        )

    def router_start(k, _):
        router_copy(k).start()
        return 0

    def router_wait(k, _):
        router_copy(k).wait()
        return 0

    barrier = pltpu.get_barrier_semaphore()

    def greet(k, _):
        to = lax.rem(flat + k, count)
        pl.semaphore_signal(
            barrier,
            inc=1,
            device_id={"owner": to // peers, "rows": lax.rem(to, peers)},
            device_id_type=MESH,
        )
        return 0

    begin(0, 0, SUBLANES)
    lax.fori_loop(1, count, greet, 0)
    largest_first[...] = jnp.zeros_like(largest_first)
    largest_rest[...] = jnp.zeros_like(largest_rest)
    row[...] = (router[...] * gain[...]).astype(row.dtype)
    maxima(0, 0, SUBLANES)
    pl.semaphore_wait(barrier, count - 1)
    scatter(0)
    begin(0, 0, 2)
    reduce(0)
    gathered(0)
    bulk(0, 0, 2, 1)
    if experts > SUBLANES:
        begin(0, SUBLANES, experts - SUBLANES)
        maxima(0, SUBLANES, experts - SUBLANES)
    begin(1, 0, experts)
    maxima(1, 0, experts)
    scatter(1)
    begin(0, 2, 2)
    bulk(0, 2, 2, 2)
    begin(0, 4, SUBLANES - 4)
    reduce(1)
    bulk(0, 4, SUBLANES - 4, PER_SEND)
    if experts > SUBLANES:
        begin(0, SUBLANES, experts - SUBLANES)
    gathered(1)
    if experts > SUBLANES:
        bulk(0, SUBLANES, experts - SUBLANES, PER_SEND)
    begin(1, 0, experts)
    lax.fori_loop(1, count, router_start, 0)
    keep_router = pltpu.make_async_copy(row, block, router_send.at[0])
    keep_router.start()
    bulk(1, 0, experts, PER_SEND)

    keep_router.wait()
    lax.fori_loop(1, count, router_wait, 0)
    for m in range(2):
        keep_copy(m, 0, experts).wait()
        for k in range(1, peers):
            send_copy(m, k, 0, experts).wait()


def land(*refs):
    arrays = len(refs) // 2
    ins, outs, sem = refs[:arrays], refs[arrays:-1], refs[-1]
    copies = [pltpu.make_async_copy(a, b, sem.at[i]) for i, (a, b) in enumerate(zip(ins, outs))]
    for copy in copies:
        copy.start()
    for copy in copies:
        copy.wait()


def fused(owners, peers, master_gate, master_up, router_weight, router_gain):
    experts, rows, width = master_gate.shape
    cut = width // peers
    tiles = width // LANES
    groups = 2 * experts // SUBLANES
    first, rest = -(-tiles // peers), -(-(groups - 1) * tiles // peers)
    depth = router_weight.shape[1]
    anywhere = pl.BlockSpec(memory_space=pl.ANY)
    vmem = pl.BlockSpec(memory_space=pltpu.VMEM)
    dma = pltpu.SemaphoreType.DMA
    turned = jax.ShapeDtypeStruct((experts, cut, rows * peers), jnp.bfloat16)

    def maxima(*shape):
        return (*shape, SUBLANES, LANES)

    gate, up, router, scales_first, scales_rest = pl.pallas_call(
        functools.partial(kernel, owners, peers),
        out_shape=(
            turned,
            turned,
            jax.ShapeDtypeStruct((depth * owners, rows * peers), jnp.bfloat16),
            jax.ShapeDtypeStruct(maxima(first * peers), jnp.float32),
            jax.ShapeDtypeStruct(maxima(rest * peers), jnp.float32),
        ),
        in_specs=[anywhere, anywhere, vmem, vmem],
        out_specs=(anywhere, anywhere, anywhere, vmem, vmem),
        scratch_shapes=[
            pltpu.VMEM((SLOTS, rows, width), jnp.float32),
            pltpu.VMEM(maxima(first * peers), jnp.float32),
            pltpu.VMEM(maxima(rest * peers), jnp.float32),
            pltpu.VMEM(maxima(peers, first), jnp.float32),
            pltpu.VMEM(maxima(peers, rest), jnp.float32),
            pltpu.VMEM((2, experts, width, rows), jnp.bfloat16),
            pltpu.VMEM((depth, rows), jnp.bfloat16),
            dma((SLOTS,)),
            dma((2, peers)),
            dma((2, peers)),
            dma((2, peers)),
            dma((2, peers)),
            dma((2, peers)),
            dma((2, peers)),
            dma((owners * peers,)),
            dma((owners * peers,)),
        ],
        compiler_params=pltpu.CompilerParams(
            collective_id=0,
            has_side_effects=True,
            vmem_limit_bytes=(4 * experts + 4 * SLOTS) * rows * width + VMEM_FOR_REST,
        ),
    )(master_gate, master_up, router_weight.T, router_gain[None, :])
    landed = (gate, up, router, scales_first, scales_rest)
    gate, up, router, scales_first, scales_rest = pl.pallas_call(
        land,
        out_shape=[jax.ShapeDtypeStruct(a.shape, a.dtype) for a in landed],
        in_specs=[anywhere] * len(landed),
        out_specs=[pl.BlockSpec(memory_space=pltpu.HBM)] * len(landed),
        scratch_shapes=[dma((len(landed),))],
        compiler_params=pltpu.CompilerParams(vmem_limit_bytes=VMEM_FOR_REST),
        cost_estimate=pl.CostEstimate(
            flops=0, bytes_accessed=2 * sum(a.size for a in landed), transcendentals=0
        ),
    )(*landed)
    scales = jnp.concatenate([scales_first[:tiles], scales_rest[: (groups - 1) * tiles]])
    scales = scales.reshape(2, experts // SUBLANES, tiles, SUBLANES, LANES)
    scales = scales.transpose(0, 1, 3, 2, 4).reshape(2, experts, width)
    scales = lax.dynamic_slice_in_dim(scales, lax.axis_index("rows") * cut, cut, axis=2)
    return (
        gate.transpose(0, 2, 1),
        up.transpose(0, 2, 1),
        scales[0],
        scales[1],
        router.T,
    )


def plain(master_gate, master_up, router_weight, router_gain):
    scale_gate, scale_up = lax.pmax(
        (jnp.max(jnp.abs(master_gate), axis=1), jnp.max(jnp.abs(master_up), axis=1)), "rows"
    )
    narrow_gate, narrow_up = (
        (master_gate / jnp.expand_dims(scale_gate, 1)).astype(jnp.bfloat16),
        (master_up / jnp.expand_dims(scale_up, 1)).astype(jnp.bfloat16),
    )
    final_gate, final_up = (
        lax.all_to_all(narrow_gate, "rows", split_axis=2, concat_axis=1, tiled=True),
        lax.all_to_all(narrow_up, "rows", split_axis=2, concat_axis=1, tiled=True),
    )
    scale_gate = lax.dynamic_slice_in_dim(
        scale_gate, lax.axis_index("rows") * final_gate.shape[2], final_gate.shape[2], axis=1
    )
    scale_up = lax.dynamic_slice_in_dim(
        scale_up, lax.axis_index("rows") * final_up.shape[2], final_up.shape[2], axis=1
    )
    part_router = (router_weight * router_gain[:, None]).astype(jnp.bfloat16)
    row_router = lax.all_gather(part_router, "rows", axis=0, tiled=True)
    serve_router = lax.all_gather(row_router, "owner", axis=1, tiled=True)
    return (final_gate, final_up, scale_gate, scale_up, serve_router)


def solution(mesh):
    owners, peers = mesh.shape["owner"], mesh.shape["rows"]

    def shards(master_gate, master_up, router_weight, router_gain):
        experts, rows, width = master_gate.shape
        whole_tiles = (
            rows % LANES == 0
            and width % LANES == 0
            and width % (peers * PACKED) == 0
            and experts % SUBLANES == 0
            and experts >= SLOTS
            and experts % PER_SEND == 0
            and router_weight.shape[1] % PACKED == 0
            and (4 * experts + 4 * SLOTS) * rows * width <= VMEM_FOR_BLOCKS
        )
        run = functools.partial(fused, owners, peers) if whole_tiles else plain
        return run(master_gate, master_up, router_weight, router_gain)

    return jax.shard_map(
        shards,
        mesh=mesh,
        in_specs=(
            P("owner", "rows", None),
            P("owner", "rows", None),
            P("rows", "owner"),
            P("rows"),
        ),
        out_specs=(
            P("owner", None, "rows"),
            P("owner", None, "rows"),
            P("owner", "rows"),
            P("owner", "rows"),
            P(),
        ),
        check_vma=False,
    )
```

profile of v0, /device:TPU:15, one launch (start us, length us, event | category | flops | bytes accessed | tf_op | source)
XLA Modules:
  0.0 533.1 jit_solution(1459124681674416077)
XLA Ops:
  0.6 0.0 copy-start
  0.6 0.7 copy-done
  1.4 0.0 copy-start.1
  1.4 0.7 copy-done.1
  2.0 522.0 %shard_map.83 = (bf16[16,176,2048]{2,1,0:T(8,128)(2,1)S(1)}, bf16[16,176,2048]{2,1,0:T(8,128)(2,1)S(1)}, bf16[64,2048]{1,0:T(8,128)(2,1)S(1)}, f32[16,8,128]{2,1,0:T(8,128)S(1)}, f32[40,8,128]{2,1,0:T(8,128)S(1)}) custom-call(f32[16,256,1408]{2,1,0:T(8,128)} %gate.1, f32[16,256,1408]{2,1,0:T(8,128)} %up.1, f32[16,256]{1,0:T(8,128)S(1)} %bitcast.14, ...), custom_call_target="tpu_custom_call" | custom-call | tf_op jit(solution)/shard_map/pallas_call | solution.py:292
  524.1 8.3 %shard_map.84 = (bf16[16,176,2048]{2,1,0:T(8,128)(2,1)}, bf16[16,176,2048]{2,1,0:T(8,128)(2,1)}, bf16[64,2048]{1,0:T(8,128)(2,1)}, f32[16,8,128]{2,1,0:T(8,128)S(1)}, f32[40,8,128]{2,1,0:T(8,128)S(1)}) custom-call(bf16[16,176,2048]{2,1,0:T(8,128)(2,1)S(1)} %get-tuple-element.15.refs_0_, bf16[16,176,2048]{2,1,0:T(8,128)(2,1)S(1)} %get-tuple-element.16.refs_1_, ...), custom_call_target="tpu_custom_call" | custom-call | bytes 23445504 | tf_op jit(solution)/shard_map/pallas_call | solution.py:328
  532.4 0.7 dynamic-slice_bitcast_fusion
  (3 shorter events, 0.0 us)
Async XLA Ops:
  0.6 0.7 copy-start
  1.4 0.7 copy-start.1
where the time goes:
time: 536 us; the launch traced here: 533 us
  Pallas kernels  530 us (99%)
    pallas_call x1, Pallas kernels, fused(): pl.pallas_call(functools.partial(kernel, owners, peers), out_shape=(turne...  522 us

commit v1 on v0

v1 whole, which is shorter than its diff:
```python
import functools

import jax
import jax.numpy as jnp
from jax import lax
from jax.experimental import pallas as pl
from jax.experimental.pallas import tpu as pltpu
from jax.sharding import PartitionSpec as P

MESH = pl.DeviceIdType.MESH
LANES = 128
SUBLANES = 8
PACKED = 16
SLOTS = 5
DIRECT = 3
LANDINGS = 4
VMEM_FOR_BLOCKS = 48 * 1024 * 1024
VMEM_FOR_REST = 2 * 1024 * 1024


def kernel(
    owners,
    peers,
    gate,
    up,
    router_hbm,
    gain_hbm,
    out_gate,
    out_up,
    out_router,
    out_scale_gate,
    out_scale_up,
    slots,
    seen,
    opening,
    largest_first,
    largest_rest,
    scales_first,
    scales_rest,
    parts_first,
    parts_rest,
    partial_first,
    partial_rest,
    across_first,
    across_rest,
    send,
    router,
    gain,
    row,
    slot_sem,
    small_sem,
    send_sem,
    recv_sem,
    seen_send,
    seen_recv,
    part_send,
    part_recv,
    across_send,
    across_recv,
    whole_send,
    whole_recv,
    router_send,
    router_recv,
):
    owner, me = lax.axis_index("owner"), lax.axis_index("rows")
    experts, rows, width = gate.shape
    tiles = width // LANES
    cut = width // peers
    near = peers // 2
    spot = lax.rem(me, near)
    masters, outs = (gate, up), (out_gate, out_up)
    largest, parts = (largest_first, largest_rest), (parts_first, parts_rest)
    partial, across = (partial_first, partial_rest), (across_first, across_rest)
    scales = (scales_first, scales_rest)
    lanes = pl.ds(pl.multiple_of(me * rows, LANES), rows)

    def partner(k):
        bits = [1 << b for b in range(peers.bit_length() - 1) if k >> b & 1]
        return sum((bit - 2 * bit * lax.rem(me // bit, 2) for bit in bits), me)

    def remote(src, dst, sent, received, to):
        return pltpu.make_async_remote_copy(
            src_ref=src,
            dst_ref=dst,
            send_sem=sent,
            recv_sem=received,
            device_id=to,
            device_id_type=MESH,
        )

    stream = [(0, 0, SUBLANES), (0, 0, DIRECT - 1)]
    if experts > SUBLANES:
        stream.append((0, SUBLANES, experts - SUBLANES))
    stream += [(1, 0, experts), (0, DIRECT - 1, experts - DIRECT + 1), (1, 0, experts)]
    bases = [sum(length for _, _, length in stream[:q]) for q in range(len(stream))]
    total = sum(length for _, _, length in stream)

    def fetch(m, e, i):
        s = lax.rem(i, SLOTS)
        return pltpu.make_async_copy(masters[m].at[e], slots.at[s], slot_sem.at[s])

    def fetch_start(i):
        for (m, first, length), base in zip(stream, bases):
            if isinstance(i, int):
                if base <= i < base + length:
                    fetch(m, first + i - base, i).start()
            else:

                @pl.when(jnp.logical_and(i >= base, i < base + length))
                def _():
                    fetch(m, first + i - base, i).start()

    def arrived(q, i):
        m, first, _ = stream[q]
        fetch(m, first + i, bases[q] + i).wait()
        return first + i, lax.rem(bases[q] + i, SLOTS)

    def following(q, i, steps):
        ahead = bases[q] + i + SLOTS
        low = bases[q] + SLOTS
        for (m, first, length), base in zip(stream, bases):
            if base + length <= low or base >= low + steps:
                continue
            if base <= low and base + length >= low + steps:
                fetch(m, first + ahead - base, ahead).start()
            else:

                @pl.when(jnp.logical_and(ahead >= base, ahead < base + length))
                def _():
                    fetch(m, first + ahead - base, ahead).start()

    def spots(m, e, c, first):
        k = m * experts + e - (0 if first else SUBLANES)
        return (k // SUBLANES) * tiles + c, pl.ds(k % SUBLANES if isinstance(k, int) else lax.rem(k, SUBLANES), 1)

    def measure(m, e, s, first):
        found = []
        for c in range(tiles):
            x = slots[s, :, c * LANES : (c + 1) * LANES]
            tile, sub = spots(m, e, c, first)
            found.append(jnp.max(jnp.abs(x), axis=0, keepdims=True))
            largest[0 if first else 1][tile, sub, :] = found[-1]
        return found

    def maxima(q, start, first):
        m, _, length = stream[q]

        def body(i, _):
            e, s = arrived(q, i)
            measure(m, e, s, first)
            following(q, i, length)
            return 0

        lax.fori_loop(start, length, body, 0)

    def seen_copy(e, k):
        return remote(
            seen.at[e, 0, pl.ds(0, tiles)],
            seen.at[e, k, pl.ds(0, tiles)],
            seen_send.at[e, k],
            seen_recv.at[e, k],
            {"rows": partner(k)},
        )

    def part_copy(stage, k):
        per = parts[stage].shape[1]
        to = partner(k)
        return remote(
            largest[stage].at[pl.ds(lax.rem(to, near) * per, per)],
            parts[stage].at[k],
            part_send.at[stage, k],
            part_recv.at[stage, k],
            {"rows": to},
        )

    def across_copy(stage):
        return remote(
            partial[stage],
            across[stage],
            across_send.at[stage],
            across_recv.at[stage],
            {"rows": partner(near)},
        )

    def share(stage, of):
        per = parts[stage].shape[1]
        return scales[stage].at[pl.ds(of * per, per)]

    def whole_copy(stage, k):
        return remote(
            share(stage, spot),
            share(stage, spot),
            whole_send.at[stage, k],
            whole_recv.at[stage, k],
            {"rows": partner(k)},
        )

    def scatter(stage):
        for k in range(1, near):
            part_copy(stage, k).start()

    def reduce(stage):
        per = parts[stage].shape[1]
        most = largest[stage][pl.ds(spot * per, per)]
        for k in range(1, near):
            part_copy(stage, k).wait_recv()
            most = jnp.maximum(most, parts[stage][k])
        partial[stage][...] = most
        across_copy(stage).start()

    def spread(stage):
        across_copy(stage).wait_recv()
        share(stage, spot)[...] = jnp.maximum(partial[stage][...], across[stage][...])
        for k in range(1, near):
            whole_copy(stage, k).start()

    def gathered(stage):
        across_copy(stage).wait_send()
        for k in range(1, near):
            part_copy(stage, k).wait_send()
            there = share(stage, lax.rem(partner(k), near))
            pltpu.make_async_copy(there, there, whole_recv.at[stage, k]).wait()
            whole_copy(stage, k).wait_send()

    def send_copy(m, k, e, length):
        to = partner(k)
        return remote(
            send.at[m, pl.ds(e, length), pl.ds(pl.multiple_of(to * cut, PACKED), cut), :],
            outs[m].at[pl.ds(e, length), :, lanes],
            send_sem.at[m, k],
            recv_sem.at[m, k],
            {"rows": to},
        )

    def keep_copy(m, e, length):
        return pltpu.make_async_copy(
            send.at[m, pl.ds(e, length), pl.ds(pl.multiple_of(me * cut, PACKED), cut), :],
            outs[m].at[pl.ds(e, length), :, lanes],
            send_sem.at[m, 0],
        )

    def one(m, e, s, scale_of):
        for c in range(tiles):
            x = slots[s, :, c * LANES : (c + 1) * LANES]
            send[m, e, c * LANES : (c + 1) * LANES, :] = (x / scale_of(c)).T.astype(send.dtype)
        for k in range(1, peers):
            send_copy(m, k, e, 1).start()
        keep_copy(m, e, 1).start()

    def bulk(q, start, stop, first):
        m, _, _ = stream[q]

        def body(i, _):
            e, s = arrived(q, i)

            def scale_of(c):
                tile, sub = spots(m, e, c, first)
                return scales[0 if first else 1][tile, sub, :]

            one(m, e, s, scale_of)
            following(q, i, stream[q][2])
            return 0

        lax.fori_loop(start, stop, body, 0)

    def early(q, i):
        e = stream[q][1] + i
        for k in range(1, peers):
            seen_copy(e, k).wait_recv()
        opening[e, :tiles, :] = jnp.max(seen[e, :, :tiles, :], axis=0)
        _, s = arrived(q, i)
        one(0, e, s, lambda c: opening[e, c : c + 1, :])
        fetch_start(bases[q] + i + SLOTS)

    depth = router.shape[0]
    mine = pl.ds(pl.multiple_of(owner * depth, PACKED), depth)

    def block(of):
        return out_router.at[mine, pl.ds(pl.multiple_of(of * rows, LANES), rows)]

    def router_across():
        return remote(row, block(me), router_send.at[0], router_recv.at[0], {"rows": partner(near)})

    def router_near(k, far):
        of = partner(near) if far else me
        return remote(
            block(of) if far else row,
            block(of),
            router_send.at[1 + 2 * k + far],
            router_recv.at[1 + 2 * k + far],
            {"rows": partner(k)},
        )

    def router_near_arrival(k, far):
        there = block(partner(near + k) if far else partner(k))
        return pltpu.make_async_copy(there, there, router_recv.at[1 + 2 * k + far])

    def router_owner(j):
        return remote(
            out_router.at[mine],
            out_router.at[mine],
            router_send.at[peers + j],
            router_recv.at[peers + j],
            {"owner": lax.rem(owner + j, owners)},
        )

    def router_owner_arrival(j):
        from_owner = lax.rem(owner + owners - j, owners)
        there = out_router.at[pl.ds(pl.multiple_of(from_owner * depth, PACKED), depth)]
        return pltpu.make_async_copy(there, there, router_recv.at[peers + j])

    barrier = pltpu.get_barrier_semaphore()

    fetch_start(0)
    for k in range(1, peers):
        pl.semaphore_signal(barrier, inc=1, device_id={"rows": partner(k)}, device_id_type=MESH)
    for j in range(1, owners):
        pl.semaphore_signal(
            barrier,
            inc=1,
            device_id={"owner": lax.rem(owner + j, owners)},
            device_id_type=MESH,
        )
    for i in range(1, SLOTS):
        fetch_start(i)
    smalls = [
        pltpu.make_async_copy(router_hbm, router, small_sem.at[0]),
        pltpu.make_async_copy(gain_hbm, gain, small_sem.at[1]),
    ]
    for copy in smalls:
        copy.start()
    largest_first[...] = jnp.zeros_like(largest_first)
    largest_rest[...] = jnp.zeros_like(largest_rest)
    for e in range(DIRECT):
        _, s = arrived(0, e)
        found = measure(0, e, s, True)
        for c in range(tiles):
            seen[e, 0, c : c + 1, :] = found[c]
        if e == 0:
            pl.semaphore_wait(barrier, peers - 1 + owners - 1)
        for k in range(1, peers):
            seen_copy(e, k).start()
        fetch_start(e + SLOTS)
    for copy in smalls:
        copy.wait()
    row[...] = (router[...] * gain[...]).astype(row.dtype)
    router_across().start()
    keep_router = pltpu.make_async_copy(row, block(me), small_sem.at[0])
    keep_router.start()
    maxima(0, DIRECT, True)
    scatter(0)
    early(1, 0)
    reduce(0)
    early(1, 1)
    rest = 2
    if experts > SUBLANES:
        maxima(rest, 0, False)
        rest += 1
    maxima(rest, 0, False)
    rest += 1
    router_across().wait_recv()
    for k in range(1, near):
        router_near(k, 0).start()
        router_near(k, 1).start()
    spread(0)
    scatter(1)
    early(rest, 0)
    gathered(0)
    bulk(rest, 1, 2, True)
    reduce(1)
    bulk(rest, 2, 3, True)
    spread(1)
    bulk(rest, 3, SUBLANES - DIRECT + 1, True)
    gathered(1)
    if experts > SUBLANES:
        bulk(rest, SUBLANES - DIRECT + 1, experts - DIRECT + 1, False)
    keep_router.wait()
    router_across().wait_send()
    for k in range(1, near):
        for far in range(2):
            router_near_arrival(k, far).wait()
            router_near(k, far).wait_send()
    for j in range(1, owners):
        router_owner(j).start()
    bulk(rest + 1, 0, experts, False)

    for at in range(peers):

        @pl.when(me == at)
        def _():
            low = at * cut // LANES
            high = -(-(at + 1) * cut // LANES)
            for m in range(2):
                for e in range(0, experts, SUBLANES):
                    first = m == 0 and e == 0
                    found = []
                    for c in range(low, high):
                        k = m * experts + e - (0 if first else SUBLANES)
                        found.append(scales[0 if first else 1][(k // SUBLANES) * tiles + c])
                    found = jnp.concatenate(found, axis=1)
                    begin = at * cut - low * LANES
                    out = (out_scale_gate, out_scale_up)[m]
                    out[e : e + SUBLANES, :] = found[:, begin : begin + cut]

    for e in range(DIRECT):
        for k in range(1, peers):
            seen_copy(e, k).wait_send()
    for j in range(1, owners):
        router_owner_arrival(j).wait()
        router_owner(j).wait_send()
    for m in range(2):
        keep_copy(m, 0, experts).wait()
        for k in range(1, peers):
            send_copy(m, k, 0, experts).wait()


def land(*refs):
    arrays = len(refs) // 2
    ins, outs, sem = refs[:arrays], refs[arrays:-1], refs[-1]
    for i, (a, b) in enumerate(zip(ins, outs)):
        pieces = LANDINGS if a.shape[0] % LANDINGS == 0 and len(a.shape) == 3 else 1
        per = a.shape[0] // pieces
        for j in range(pieces):
            at = pl.ds(j * per, per)
            pltpu.make_async_copy(a.at[at], b.at[at], sem.at[i]).start()
    for i, (a, b) in enumerate(zip(ins, outs)):
        pltpu.make_async_copy(a, b, sem.at[i]).wait()


def fused(owners, peers, master_gate, master_up, router_weight, router_gain):
    experts, rows, width = master_gate.shape
    cut = width // peers
    near = peers // 2
    tiles = width // LANES
    padded = -(-tiles // SUBLANES) * SUBLANES
    groups = 2 * experts // SUBLANES
    first, rest = -(-tiles // near), -(-(groups - 1) * tiles // near)
    depth = router_weight.shape[1]
    anywhere = pl.BlockSpec(memory_space=pl.ANY)
    vmem = pl.BlockSpec(memory_space=pltpu.VMEM)
    hbm = pl.BlockSpec(memory_space=pltpu.HBM)
    dma = pltpu.SemaphoreType.DMA
    turned = jax.ShapeDtypeStruct((experts, cut, rows * peers), jnp.bfloat16)
    scale = jax.ShapeDtypeStruct((experts, cut), jnp.float32)

    def maxima(*shape):
        return pltpu.VMEM((*shape, SUBLANES, LANES), jnp.float32)

    landed = pl.pallas_call(
        functools.partial(kernel, owners, peers),
        out_shape=(
            turned,
            turned,
            jax.ShapeDtypeStruct((depth * owners, rows * peers), jnp.bfloat16),
            scale,
            scale,
        ),
        in_specs=[anywhere, anywhere, hbm, hbm],
        out_specs=(anywhere, anywhere, anywhere, vmem, vmem),
        scratch_shapes=[
            pltpu.VMEM((SLOTS, rows, width), jnp.float32),
            pltpu.VMEM((DIRECT, peers, padded, LANES), jnp.float32),
            pltpu.VMEM((DIRECT, padded, LANES), jnp.float32),
            maxima(first * near),
            maxima(rest * near),
            maxima(first * near),
            maxima(rest * near),
            maxima(near, first),
            maxima(near, rest),
            maxima(first),
            maxima(rest),
            maxima(first),
            maxima(rest),
            pltpu.VMEM((2, experts, width, rows), jnp.bfloat16),
            pltpu.VMEM((depth, rows), jnp.float32),
            pltpu.VMEM((1, rows), jnp.float32),
            pltpu.VMEM((depth, rows), jnp.bfloat16),
            dma((SLOTS,)),
            dma((2,)),
            dma((2, peers)),
            dma((2, peers)),
            dma((DIRECT, peers)),
            dma((DIRECT, peers)),
            dma((2, near)),
            dma((2, near)),
            dma((2,)),
            dma((2,)),
            dma((2, near)),
            dma((2, near)),
            dma((peers + owners,)),
            dma((peers + owners,)),
        ],
        compiler_params=pltpu.CompilerParams(
            collective_id=0,
            has_side_effects=True,
            vmem_limit_bytes=(4 * experts + 4 * SLOTS) * rows * width + VMEM_FOR_REST,
        ),
    )(master_gate, master_up, *(pltpu.with_memory_space_constraint(a, pltpu.HBM) for a in (router_weight.T, router_gain[None, :])))
    gate, up, router, scale_gate, scale_up = pl.pallas_call(
        land,
        out_shape=[jax.ShapeDtypeStruct(a.shape, a.dtype) for a in landed],
        in_specs=[anywhere] * len(landed),
        out_specs=[hbm] * len(landed),
        scratch_shapes=[dma((len(landed),))],
        compiler_params=pltpu.CompilerParams(vmem_limit_bytes=VMEM_FOR_REST),
        cost_estimate=pl.CostEstimate(
            flops=0, bytes_accessed=2 * sum(a.size for a in landed), transcendentals=0
        ),
    )(*landed)
    return gate.transpose(0, 2, 1), up.transpose(0, 2, 1), scale_gate, scale_up, router.T


def plain(master_gate, master_up, router_weight, router_gain):
    scale_gate, scale_up = lax.pmax(
        (jnp.max(jnp.abs(master_gate), axis=1), jnp.max(jnp.abs(master_up), axis=1)), "rows"
    )
    narrow_gate, narrow_up = (
        (master_gate / jnp.expand_dims(scale_gate, 1)).astype(jnp.bfloat16),
        (master_up / jnp.expand_dims(scale_up, 1)).astype(jnp.bfloat16),
    )
    final_gate, final_up = (
        lax.all_to_all(narrow_gate, "rows", split_axis=2, concat_axis=1, tiled=True),
        lax.all_to_all(narrow_up, "rows", split_axis=2, concat_axis=1, tiled=True),
    )
    scale_gate = lax.dynamic_slice_in_dim(
        scale_gate, lax.axis_index("rows") * final_gate.shape[2], final_gate.shape[2], axis=1
    )
    scale_up = lax.dynamic_slice_in_dim(
        scale_up, lax.axis_index("rows") * final_up.shape[2], final_up.shape[2], axis=1
    )
    part_router = (router_weight * router_gain[:, None]).astype(jnp.bfloat16)
    row_router = lax.all_gather(part_router, "rows", axis=0, tiled=True)
    serve_router = lax.all_gather(row_router, "owner", axis=1, tiled=True)
    return (final_gate, final_up, scale_gate, scale_up, serve_router)


def solution(mesh):
    owners, peers = mesh.shape["owner"], mesh.shape["rows"]

    def shards(master_gate, master_up, router_weight, router_gain):
        experts, rows, width = master_gate.shape
        whole_tiles = (
            peers & (peers - 1) == 0
            and peers > 2
            and rows % LANES == 0
            and width % LANES == 0
            and width % (peers * PACKED) == 0
            and experts % SUBLANES == 0
            and router_weight.shape[1] % PACKED == 0
            and (4 * experts + 4 * SLOTS) * rows * width <= VMEM_FOR_BLOCKS
        )
        run = functools.partial(fused, owners, peers) if whole_tiles else plain
        return run(master_gate, master_up, router_weight, router_gain)

    return jax.shard_map(
        shards,
        mesh=mesh,
        in_specs=(
            P("owner", "rows", None),
            P("owner", "rows", None),
            P("rows", "owner"),
            P("rows"),
        ),
        out_specs=(
            P("owner", None, "rows"),
            P("owner", None, "rows"),
            P("owner", "rows"),
            P("owner", "rows"),
            P(),
        ),
        check_vma=False,
    )
```

time: 536 us -> 517 us (0.965)
  Pallas kernels: 530 us -> 512 us
    pallas_call x1, Pallas kernels: 522 us -> 504 us  [fused(): pl.pallas_call(functools.partial(kernel, owners, peers), out_shape=(turne...]
where the time goes in v1:
time: 517 us; the launch traced here: 512 us
  Pallas kernels  512 us (99%)
    pallas_call x1, Pallas kernels, fused(): pl.pallas_call(functools.partial(kernel, owners, peers), out_shape=(turne...  504 us

profile of v1, /device:TPU:15, one launch (start us, length us, event | category | flops | bytes accessed | tf_op | source)
XLA Modules:
  0.0 512.4 jit_solution(4934321050042706736)
XLA Ops:
  0.6 503.8 %shard_map.83 = (bf16[16,176,2048]{2,1,0:T(8,128)(2,1)S(1)}, bf16[16,176,2048]{2,1,0:T(8,128)(2,1)S(1)}, bf16[64,2048]{1,0:T(8,128)(2,1)S(1)}, f32[16,176]{1,0:T(8,128)S(1)}, f32[16,176]{1,0:T(8,128)S(1)}) custom-call(f32[16,256,1408]{2,1,0:T(8,128)} %gate.1, f32[16,256,1408]{2,1,0:T(8,128)} %up.1, f32[16,256]{1,0:T(8,128)} %bitcast.5, f32[1,256]{1,0:T(1,128)} %bitcast.6), custom_call_target="tpu_custom_call" | custom-call | tf_op jit(solution)/shard_map/pallas_call | solution.py:449
  504.5 7.9 %shard_map.84 = (bf16[16,176,2048]{2,1,0:T(8,128)(2,1)}, bf16[16,176,2048]{2,1,0:T(8,128)(2,1)}, bf16[64,2048]{1,0:T(8,128)(2,1)}, f32[16,176]{1,0:T(8,128)}, f32[16,176]{1,0:T(8,128)}) custom-call(bf16[16,176,2048]{2,1,0:T(8,128)(2,1)S(1)} %get-tuple-element.15.refs_0_, bf16[16,176,2048]{2,1,0:T(8,128)(2,1)S(1)} %get-tuple-element.16.refs_1_, ...), custom_call_target="tpu_custom_call" | custom-call | bytes 23342080 | tf_op jit(solution)/shard_map/pallas_call | solution.py:499

commit v2 on v1

--- a/solution.py
+++ b/solution.py
@@ -12,10 +12,18 @@
 SUBLANES = 8
 PACKED = 16
 SLOTS = 5
-DIRECT = 3
+DIRECT = 2
+LATER = (0, 3)
 LANDINGS = 4
 VMEM_FOR_BLOCKS = 48 * 1024 * 1024
 VMEM_FOR_REST = 2 * 1024 * 1024
+
+
+def half(lower, tiles, far):
+    count = -(-tiles // 2)
+    if far:
+        return jnp.where(lower, tiles - count, 0), count
+    return jnp.where(lower, 0, count), tiles - count
 
 
 def kernel(
@@ -30,13 +38,13 @@
     out_router,
     out_scale_gate,
     out_scale_up,
+    scales_rest,
     slots,
     seen,
     opening,
     largest_first,
     largest_rest,
     scales_first,
-    scales_rest,
     parts_first,
     parts_rest,
     partial_first,
@@ -88,10 +96,11 @@
             device_id_type=MESH,
         )
 
-    stream = [(0, 0, SUBLANES), (0, 0, DIRECT - 1)]
+    stream = [(0, 0, SUBLANES), (0, 0, DIRECT)]
     if experts > SUBLANES:
         stream.append((0, SUBLANES, experts - SUBLANES))
-    stream += [(1, 0, experts), (0, DIRECT - 1, experts - DIRECT + 1), (1, 0, experts)]
+    stream += [(1, 0, experts), (0, DIRECT, experts - DIRECT)]
+    stream.append((1, 0, experts - max(LATER)))
     bases = [sum(length for _, _, length in stream[:q]) for q in range(len(stream))]
     total = sum(length for _, _, length in stream)
 
@@ -239,12 +248,17 @@
             send_sem.at[m, 0],
         )
 
-    def one(m, e, s, scale_of):
-        for c in range(tiles):
-            x = slots[s, :, c * LANES : (c + 1) * LANES]
-            send[m, e, c * LANES : (c + 1) * LANES, :] = (x / scale_of(c)).T.astype(send.dtype)
-        for k in range(1, peers):
-            send_copy(m, k, e, 1).start()
+    held = range(near + near // 2, peers)
+
+    def one(m, e, s, scale_of, hold=False):
+        for far in (True, False):
+            low, count = half(me < near, tiles, far)
+            for c in range(count):
+                at = pl.ds(pl.multiple_of((low + c) * LANES, LANES), LANES)
+                send[m, e, at, :] = (slots[s, :, at] / scale_of(low + c)).T.astype(send.dtype)
+            for k in range(near, peers) if far else range(1, near):
+                if not (hold and k in held):
+                    send_copy(m, k, e, 1).start()
         keep_copy(m, e, 1).start()
 
     def bulk(q, start, stop, first):
@@ -263,13 +277,13 @@
 
         lax.fori_loop(start, stop, body, 0)
 
-    def early(q, i):
+    def early(q, i, hold):
         e = stream[q][1] + i
         for k in range(1, peers):
             seen_copy(e, k).wait_recv()
         opening[e, :tiles, :] = jnp.max(seen[e, :, :tiles, :], axis=0)
         _, s = arrived(q, i)
-        one(0, e, s, lambda c: opening[e, c : c + 1, :])
+        one(0, e, s, lambda c: opening[e, pl.ds(c, 1), :], hold)
         fetch_start(bases[q] + i + SLOTS)
 
     depth = router.shape[0]
@@ -321,22 +335,23 @@
             device_id={"owner": lax.rem(owner + j, owners)},
             device_id_type=MESH,
         )
-    for i in range(1, SLOTS):
-        fetch_start(i)
     smalls = [
         pltpu.make_async_copy(router_hbm, router, small_sem.at[0]),
         pltpu.make_async_copy(gain_hbm, gain, small_sem.at[1]),
     ]
-    for copy in smalls:
-        copy.start()
     largest_first[...] = jnp.zeros_like(largest_first)
     largest_rest[...] = jnp.zeros_like(largest_rest)
     for e in range(DIRECT):
         _, s = arrived(0, e)
+        if e == 0:
+            for i in range(1, SLOTS):
+                fetch_start(i)
         found = measure(0, e, s, True)
         for c in range(tiles):
             seen[e, 0, c : c + 1, :] = found[c]
         if e == 0:
+            for copy in smalls:
+                copy.start()
             pl.semaphore_wait(barrier, peers - 1 + owners - 1)
         for k in range(1, peers):
             seen_copy(e, k).start()
@@ -349,9 +364,9 @@
     keep_router.start()
     maxima(0, DIRECT, True)
     scatter(0)
-    early(1, 0)
+    early(1, 0, False)
     reduce(0)
-    early(1, 1)
+    early(1, 1, True)
     rest = 2
     if experts > SUBLANES:
         maxima(rest, 0, False)
@@ -364,16 +379,17 @@
         router_near(k, 1).start()
     spread(0)
     scatter(1)
-    early(rest, 0)
+    for k in held:
+        send_copy(0, k, 1, 1).start()
     gathered(0)
+    bulk(rest, 0, 1, True)
+    reduce(1)
     bulk(rest, 1, 2, True)
-    reduce(1)
-    bulk(rest, 2, 3, True)
     spread(1)
-    bulk(rest, 3, SUBLANES - DIRECT + 1, True)
+    bulk(rest, 2, SUBLANES - DIRECT, True)
     gathered(1)
     if experts > SUBLANES:
-        bulk(rest, SUBLANES - DIRECT + 1, experts - DIRECT + 1, False)
+        bulk(rest, SUBLANES - DIRECT, experts - DIRECT, False)
     keep_router.wait()
     router_across().wait_send()
     for k in range(1, near):
@@ -382,7 +398,30 @@
             router_near(k, far).wait_send()
     for j in range(1, owners):
         router_owner(j).start()
-    bulk(rest + 1, 0, experts, False)
+    bulk(rest + 1, 0, experts - max(LATER), False)
+    for turn, later in enumerate(LATER):
+        if later == max(LATER):
+            continue
+
+        @pl.when(lax.rem(owner, len(LATER)) == turn)
+        def _():
+            extra = max(LATER) - later
+            low = experts - max(LATER)
+            for i in range(extra):
+                fetch(1, low + i, i).start()
+
+            def body(i, _):
+                fetch(1, low + i, i).wait()
+
+                def scale_of(c):
+                    tile, sub = spots(1, low + i, c, False)
+                    return scales_rest[tile, sub, :]
+
+                one(1, low + i, i, scale_of)
+                return 0
+
+            lax.fori_loop(0, extra, body, 0)
+
 
     for at in range(peers):
 
@@ -408,23 +447,145 @@
     for j in range(1, owners):
         router_owner_arrival(j).wait()
         router_owner(j).wait_send()
-    for m in range(2):
-        keep_copy(m, 0, experts).wait()
+    keep_copy(0, 0, experts).wait()
+    for k in range(1, peers):
+        send_copy(0, k, 0, experts).wait()
+    for turn, later in enumerate(LATER):
+
+        @pl.when(lax.rem(owner, len(LATER)) == turn)
+        def _():
+            keep_copy(1, 0, experts - later).wait()
+            for k in range(1, peers):
+                send_copy(1, k, 0, experts - later).wait()
+
+
+def last_kernel(peers, up, scales, out, slots, send, slot_sem, send_sem, recv_sem):
+    owner, me = lax.axis_index("owner"), lax.axis_index("rows")
+    experts, rows, width = up.shape
+    tiles = width // LANES
+    cut = width // peers
+    lanes = pl.ds(pl.multiple_of(me * rows, LANES), rows)
+    turn = lax.rem(owner, len(LATER))
+    later = sum(jnp.where(turn == t, n, 0) for t, n in enumerate(LATER))
+
+    def partner(k):
+        bits = [1 << b for b in range(peers.bit_length() - 1) if k >> b & 1]
+        return sum((bit - 2 * bit * lax.rem(me // bit, 2) for bit in bits), me)
+
+    def fetch(i):
+        return pltpu.make_async_copy(
+            up.at[experts - later + i], slots.at[i], slot_sem.at[i]
+        )
+
+    def prepare(i):
+        fetch(i).wait()
+        sub = pl.ds(SUBLANES - later + i, 1)
+        for c in range(tiles):
+            x = slots[i, :, c * LANES : (c + 1) * LANES]
+            send[i, c * LANES : (c + 1) * LANES, :] = (x / scales[c, sub, :]).T.astype(send.dtype)
+
+    def send_copy(k, i, length):
+        to = partner(k)
+        return pltpu.make_async_remote_copy(
+            src_ref=send.at[pl.ds(i, length), pl.ds(pl.multiple_of(to * cut, PACKED), cut), :],
+            dst_ref=out.at[pl.ds(i, length), :, lanes],
+            send_sem=send_sem.at[k],
+            recv_sem=recv_sem.at[k],
+            device_id={"rows": to},
+            device_id_type=MESH,
+        )
+
+    def keep_copy(i, length):
+        return pltpu.make_async_copy(
+            send.at[pl.ds(i, length), pl.ds(pl.multiple_of(me * cut, PACKED), cut), :],
+            out.at[pl.ds(i, length), :, lanes],
+            send_sem.at[0],
+        )
+
+    def post(i):
         for k in range(1, peers):
-            send_copy(m, k, 0, experts).wait()
-
-
-def land(*refs):
-    arrays = len(refs) // 2
-    ins, outs, sem = refs[:arrays], refs[arrays:-1], refs[-1]
-    for i, (a, b) in enumerate(zip(ins, outs)):
-        pieces = LANDINGS if a.shape[0] % LANDINGS == 0 and len(a.shape) == 3 else 1
-        per = a.shape[0] // pieces
-        for j in range(pieces):
-            at = pl.ds(j * per, per)
-            pltpu.make_async_copy(a.at[at], b.at[at], sem.at[i]).start()
-    for i, (a, b) in enumerate(zip(ins, outs)):
-        pltpu.make_async_copy(a, b, sem.at[i]).wait()
+            send_copy(k, i, 1).start()
+        keep_copy(i, 1).start()
+
+    barrier = pltpu.get_barrier_semaphore()
+    for k in range(1, peers):
+        pl.semaphore_signal(barrier, inc=1, device_id={"rows": partner(k)}, device_id_type=MESH)
+
+    def begin(i, _):
+        fetch(i).start()
+        return 0
+
+    lax.fori_loop(0, later, begin, 0)
+    if min(LATER) > 0:
+        prepare(0)
+    else:
+        pl.when(later > 0)(lambda: prepare(0))
+    pl.semaphore_wait(barrier, peers - 1)
+    if min(LATER) > 0:
+        post(0)
+    else:
+        pl.when(later > 0)(lambda: post(0))
+
+    def body(i, _):
+        prepare(i)
+        post(i)
+        return 0
+
+    lax.fori_loop(1, later, body, 0)
+    for t, n in enumerate(LATER):
+        if n == 0:
+            continue
+
+        @pl.when(turn == t)
+        def _():
+            keep_copy(0, n).wait()
+            for k in range(1, peers):
+                send_copy(k, 0, n).wait()
+
+
+def land(gate, up, router, scale_gate, scale_up, scales, *refs):
+    outs, last_scales, sem = refs[:5], refs[5], refs[6]
+    tiles = last_scales.shape[0]
+    experts = gate.shape[0]
+
+    def move(i, a, b, low, high, pieces):
+        cuts = [low + (high - low) * j // pieces for j in range(pieces + 1)]
+        for at, end in zip(cuts, cuts[1:]):
+            span = pl.ds(at, end - at)
+            pltpu.make_async_copy(a.at[span], b.at[span], sem.at[i]).start()
+
+    def moved(i, a, b, low, high):
+        span = pl.ds(low, high - low)
+        pltpu.make_async_copy(a.at[span], b.at[span], sem.at[i]).wait()
+
+    whole = [(0, gate), (2, router), (3, scale_gate), (4, scale_up)]
+    for i, a in whole:
+        move(i, a, outs[i], 0, a.shape[0], LANDINGS if i == 0 else 1)
+    for turn, later in enumerate(LATER):
+
+        @pl.when(lax.rem(lax.axis_index("owner"), len(LATER)) == turn)
+        def _():
+            move(1, up, outs[1], 0, experts - later, LANDINGS)
+            moved(1, up, outs[1], 0, experts - later)
+
+    low = (2 * experts // SUBLANES - 2) * tiles
+    last_scales[...] = scales[low : low + tiles]
+    for i, a in whole:
+        moved(i, a, outs[i], 0, a.shape[0])
+
+
+def last_land(_, last, up, sem):
+    experts = up.shape[0]
+    for turn, later in enumerate(LATER):
+        if later == 0:
+            continue
+
+        @pl.when(lax.rem(lax.axis_index("owner"), len(LATER)) == turn)
+        def _():
+            there = up.at[pl.ds(experts - later, later)]
+            copy = pltpu.make_async_copy(last.at[pl.ds(0, later)], there, sem)
+            copy.start()
+            copy.wait()
 
 
 def fused(owners, peers, master_gate, master_up, router_weight, router_gain):
@@ -443,6 +604,9 @@
     turned = jax.ShapeDtypeStruct((experts, cut, rows * peers), jnp.bfloat16)
     scale = jax.ShapeDtypeStruct((experts, cut), jnp.float32)
 
+    def in_hbm(a):
+        return pltpu.with_memory_space_constraint(a, pltpu.HBM)
+
     def maxima(*shape):
         return pltpu.VMEM((*shape, SUBLANES, LANES), jnp.float32)
 
@@ -454,9 +618,10 @@
             jax.ShapeDtypeStruct((depth * owners, rows * peers), jnp.bfloat16),
             scale,
             scale,
+            jax.ShapeDtypeStruct((rest * near, SUBLANES, LANES), jnp.float32),
         ),
         in_specs=[anywhere, anywhere, hbm, hbm],
-        out_specs=(anywhere, anywhere, anywhere, vmem, vmem),
+        out_specs=(anywhere, anywhere, anywhere, vmem, vmem, vmem),
         scratch_shapes=[
             pltpu.VMEM((SLOTS, rows, width), jnp.float32),
             pltpu.VMEM((DIRECT, peers, padded, LANES), jnp.float32),
@@ -464,7 +629,6 @@
             maxima(first * near),
             maxima(rest * near),
             maxima(first * near),
-            maxima(rest * near),
             maxima(near, first),
             maxima(near, rest),
             maxima(first),
@@ -495,18 +659,45 @@
             has_side_effects=True,
             vmem_limit_bytes=(4 * experts + 4 * SLOTS) * rows * width + VMEM_FOR_REST,
         ),
-    )(master_gate, master_up, *(pltpu.with_memory_space_constraint(a, pltpu.HBM) for a in (router_weight.T, router_gain[None, :])))
-    gate, up, router, scale_gate, scale_up = pl.pallas_call(
+    )(*(in_hbm(a) for a in (master_gate, master_up, router_weight.T, router_gain[None, :])))
+    local = [jax.ShapeDtypeStruct(a.shape, a.dtype) for a in landed[:5]]
+    small = pltpu.CompilerParams(vmem_limit_bytes=VMEM_FOR_REST)
+    gate, up, router, scale_gate, scale_up, scales = pl.pallas_call(
         land,
-        out_shape=[jax.ShapeDtypeStruct(a.shape, a.dtype) for a in landed],
-        in_specs=[anywhere] * len(landed),
-        out_specs=[hbm] * len(landed),
-        scratch_shapes=[dma((len(landed),))],
-        compiler_params=pltpu.CompilerParams(vmem_limit_bytes=VMEM_FOR_REST),
-        cost_estimate=pl.CostEstimate(
-            flops=0, bytes_accessed=2 * sum(a.size for a in landed), transcendentals=0
+        out_shape=[*local, jax.ShapeDtypeStruct((tiles, SUBLANES, LANES), jnp.float32)],
+        in_specs=[anywhere] * 5 + [vmem],
+        out_specs=[hbm] * 5 + [vmem],
+        scratch_shapes=[dma((5,))],
+        compiler_params=small,
+    )(*landed)
+    most = max(LATER)
+    last = pl.pallas_call(
+        functools.partial(last_kernel, peers),
+        out_shape=jax.ShapeDtypeStruct((most, cut, rows * peers), jnp.bfloat16),
+        in_specs=[anywhere, vmem],
+        out_specs=anywhere,
+        scratch_shapes=[
+            pltpu.VMEM((most, rows, width), jnp.float32),
+            pltpu.VMEM((most, width, rows), jnp.bfloat16),
+            dma((most,)),
+            dma((peers,)),
+            dma((peers,)),
+        ],
+        compiler_params=pltpu.CompilerParams(
+            collective_id=1,
+            has_side_effects=True,
+            vmem_limit_bytes=6 * most * rows * width + VMEM_FOR_REST,
         ),
-    )(*landed)
+    )(in_hbm(master_up), scales)
+    up = pl.pallas_call(
+        last_land,
+        out_shape=local[1],
+        in_specs=[hbm, anywhere],
+        out_specs=hbm,
+        scratch_shapes=[dma],
+        input_output_aliases={0: 0},
+        compiler_params=small,
+    )(up, last)
     return gate.transpose(0, 2, 1), up.transpose(0, 2, 1), scale_gate, scale_up, router.T
 
 

time: 517 us -> 509 us (0.985)
    pallas_call x1, Pallas kernels: 504 us -> 470 us  [fused(): pl.pallas_call(functools.partial(kernel, owners, peers), out_shape=(turne...]
    pallas_call x1 -> x3, Pallas kernels: 7.86 us -> 37.8 us  [the longest x1 29.2 us: fused(): pl.pallas_call(functools.partial(last_kernel, peers), out_shape=jax.Shape...]
where the time goes in v2:
time: 509 us
  Pallas kernels  508 us (100%)
    pallas_call x1, Pallas kernels, fused(): pl.pallas_call(functools.partial(kernel, owners, peers), out_shape=(turne...  470 us
    pallas_call x1, Pallas kernels, fused(): pl.pallas_call(functools.partial(last_kernel, peers), out_shape=jax.Shape...  29.2 us

profile of v2, /device:TPU:15, one launch (start us, length us, event | category | flops | bytes accessed | tf_op | source)
XLA Modules:
  0.0 508.7 jit_solution(3404387283724466570)
XLA Ops:
  0.6 470.2 %shard_map.83 = (bf16[16,176,2048]{2,1,0:T(8,128)(2,1)S(1)}, bf16[16,176,2048]{2,1,0:T(8,128)(2,1)S(1)}, bf16[64,2048]{1,0:T(8,128)(2,1)S(1)}, f32[16,176]{1,0:T...) custom-call(f32[16,256,1408]{2,1,0:T(8,128)} %gate.1, f32[16,256,1408]{2,1,0:T(8,128)} %up.3, ...), custom_call_target="tpu_custom_call" | custom-call | tf_op jit(solution)/shard_map/pallas_call | solution.py:613
  470.8 7.3 %shard_map.84 = (bf16[16,176,2048]{2,1,0:T(8,128)(2,1)}, bf16[16,176,2048]{2,1,0:T(8,128)(2,1)}, bf16[64,2048]{1,0:T(8,128)(2,1)}, f32[16,176]{1,0:T(8,128)}, f3...) custom-call(bf16[16,176,2048]{2,1,0:T(8,128)(2,1)S(1)} %get-tuple-element.17.gate, ...), custom_call_target="tpu_custom_call" | custom-call | tf_op jit(solution)/shard_map/pallas_call | solution.py:665
  478.1 29.2 %shard_map.85.last = bf16[3,176,2048]{2,1,0:T(8,128)(2,1)S(1)} custom-call(f32[16,256,1408]{2,1,0:T(8,128)} %up.3, f32[11,8,128]{2,1,0:T(8,128)S(1)} %get-tuple-element.25.scales), custom_call_target="tpu_custom_call" | custom-call | tf_op jit(solution)/shard_map/pallas_call | solution.py:674
  507.3 1.4 shard_map.86

commit v3 on v2

--- a/solution.py
+++ b/solution.py
@@ -24,6 +24,12 @@
     if far:
         return jnp.where(lower, tiles - count, 0), count
     return jnp.where(lower, 0, count), tiles - count
+
+
+def far_targets(me, peers):
+    near = peers // 2
+    base = near - near * (me // near)
+    return [base + p for p in range(near)]
 
 
 def kernel(
@@ -231,24 +237,30 @@
             pltpu.make_async_copy(there, there, whole_recv.at[stage, k]).wait()
             whole_copy(stage, k).wait_send()
 
-    def send_copy(m, k, e, length):
-        to = partner(k)
+    def send_copy(m, to, e, length):
         return remote(
             send.at[m, pl.ds(e, length), pl.ds(pl.multiple_of(to * cut, PACKED), cut), :],
             outs[m].at[pl.ds(e, length), :, lanes],
-            send_sem.at[m, k],
-            recv_sem.at[m, k],
+            send_sem.at[m, to],
+            recv_sem.at[m, me],
             {"rows": to},
         )
+
+    def sent_and_received(m, length):
+        for to in [partner(k) for k in range(1, peers)]:
+            send_copy(m, to, 0, length).wait_send()
+            there = outs[m].at[pl.ds(0, length), :, pl.ds(pl.multiple_of(to * rows, LANES), rows)]
+            pltpu.make_async_copy(there, there, recv_sem.at[m, to]).wait()
 
     def keep_copy(m, e, length):
         return pltpu.make_async_copy(
             send.at[m, pl.ds(e, length), pl.ds(pl.multiple_of(me * cut, PACKED), cut), :],
             outs[m].at[pl.ds(e, length), :, lanes],
-            send_sem.at[m, 0],
-        )
-
-    held = range(near + near // 2, peers)
+            send_sem.at[m, me],
+        )
+
+    across_from = far_targets(me, peers)
+    held = across_from[near // 2 :]
 
     def one(m, e, s, scale_of, hold=False):
         for far in (True, False):
@@ -256,9 +268,11 @@
             for c in range(count):
                 at = pl.ds(pl.multiple_of((low + c) * LANES, LANES), LANES)
                 send[m, e, at, :] = (slots[s, :, at] / scale_of(low + c)).T.astype(send.dtype)
-            for k in range(near, peers) if far else range(1, near):
-                if not (hold and k in held):
-                    send_copy(m, k, e, 1).start()
+            targets = [partner(k) for k in range(1, near)]
+            if far:
+                targets = across_from[: near // 2] if hold else across_from
+            for to in targets:
+                send_copy(m, to, e, 1).start()
         keep_copy(m, e, 1).start()
 
     def bulk(q, start, stop, first):
@@ -379,8 +393,8 @@
         router_near(k, 1).start()
     spread(0)
     scatter(1)
-    for k in held:
-        send_copy(0, k, 1, 1).start()
+    for to in held:
+        send_copy(0, to, 1, 1).start()
     gathered(0)
     bulk(rest, 0, 1, True)
     reduce(1)
@@ -448,15 +462,13 @@
         router_owner_arrival(j).wait()
         router_owner(j).wait_send()
     keep_copy(0, 0, experts).wait()
-    for k in range(1, peers):
-        send_copy(0, k, 0, experts).wait()
+    sent_and_received(0, experts)
     for turn, later in enumerate(LATER):
 
         @pl.when(lax.rem(owner, len(LATER)) == turn)
         def _():
             keep_copy(1, 0, experts - later).wait()
-            for k in range(1, peers):
-                send_copy(1, k, 0, experts - later).wait()
+            sent_and_received(1, experts - later)
 
 
 def last_kernel(peers, up, scales, out, slots, send, slot_sem, send_sem, recv_sem):
@@ -465,6 +477,7 @@
     tiles = width // LANES
     cut = width // peers
     lanes = pl.ds(pl.multiple_of(me * rows, LANES), rows)
+    near = peers // 2
     turn = lax.rem(owner, len(LATER))
     later = sum(jnp.where(turn == t, n, 0) for t, n in enumerate(LATER))
 
@@ -484,13 +497,12 @@
             x = slots[i, :, c * LANES : (c + 1) * LANES]
             send[i, c * LANES : (c + 1) * LANES, :] = (x / scales[c, sub, :]).T.astype(send.dtype)
 
-    def send_copy(k, i, length):
-        to = partner(k)
+    def send_copy(to, i, length):
         return pltpu.make_async_remote_copy(
             src_ref=send.at[pl.ds(i, length), pl.ds(pl.multiple_of(to * cut, PACKED), cut), :],
             dst_ref=out.at[pl.ds(i, length), :, lanes],
-            send_sem=send_sem.at[k],
-            recv_sem=recv_sem.at[k],
+            send_sem=send_sem.at[to],
+            recv_sem=recv_sem.at[me],
             device_id={"rows": to},
             device_id_type=MESH,
         )
@@ -499,12 +511,14 @@
         return pltpu.make_async_copy(
             send.at[pl.ds(i, length), pl.ds(pl.multiple_of(me * cut, PACKED), cut), :],
             out.at[pl.ds(i, length), :, lanes],
-            send_sem.at[0],
+            send_sem.at[me],
         )
 
     def post(i):
-        for k in range(1, peers):
-            send_copy(k, i, 1).start()
+        for k in range(1, near):
+            send_copy(partner(k), i, 1).start()
+        for to in far_targets(me, peers):
+            send_copy(to, i, 1).start()
         keep_copy(i, 1).start()
 
     barrier = pltpu.get_barrier_semaphore()
@@ -539,8 +553,10 @@
         @pl.when(turn == t)
         def _():
             keep_copy(0, n).wait()
-            for k in range(1, peers):
-                send_copy(k, 0, n).wait()
+            for to in [partner(k) for k in range(1, peers)]:
+                send_copy(to, 0, n).wait_send()
+                there = out.at[pl.ds(0, n), :, pl.ds(pl.multiple_of(to * rows, LANES), rows)]
+                pltpu.make_async_copy(there, there, recv_sem.at[to]).wait()
 
 
 def land(gate, up, router, scale_gate, scale_up, scales, *refs):

time: 509 us -> 508 us (level)
  no operation moved by 1% of the time
where the time goes in v3:
time: 508 us
  Pallas kernels  507 us (100%)
    pallas_call x1, Pallas kernels, fused(): pl.pallas_call(functools.partial(kernel, owners, peers), out_shape=(turne...  471 us
    pallas_call x1, Pallas kernels, fused(): pl.pallas_call(functools.partial(last_kernel, peers), out_shape=jax.Shape...  27.4 us

profile of v3, /device:TPU:15, one launch (start us, length us, event | category | flops | bytes accessed | tf_op | source)
XLA Modules:
  0.0 507.6 jit_solution(12181050524636107464)
XLA Ops:
  0.6 470.9 %shard_map.83 = (bf16[16,176,2048]{2,1,0:T(8,128)(2,1)S(1)}, bf16[16,176,2048]{2,1,0:T(8,128)(2,1)S(1)}, bf16[64,2048]{1,0:T(8,128)(2,1)S(1)}, f32[16,176]{1,0:T...) custom-call(f32[16,256,1408]{2,1,0:T(8,128)} %gate.1, f32[16,256,1408]{2,1,0:T(8,128)} %up.3, ...), custom_call_target="tpu_custom_call" | custom-call | tf_op jit(solution)/shard_map/pallas_call | solution.py:629
  471.5 7.3 %shard_map.84 = (bf16[16,176,2048]{2,1,0:T(8,128)(2,1)}, bf16[16,176,2048]{2,1,0:T(8,128)(2,1)}, bf16[64,2048]{1,0:T(8,128)(2,1)}, f32[16,176]{1,0:T(8,128)}, f3...) custom-call(bf16[16,176,2048]{2,1,0:T(8,128)(2,1)S(1)} %get-tuple-element.17.gate, ...), custom_call_target="tpu_custom_call" | custom-call | tf_op jit(solution)/shard_map/pallas_call | solution.py:681
  478.8 27.4 %shard_map.85.last = bf16[3,176,2048]{2,1,0:T(8,128)(2,1)S(1)} custom-call(f32[16,256,1408]{2,1,0:T(8,128)} %up.3, f32[11,8,128]{2,1,0:T(8,128)S(1)} %get-tuple-element.25.scales), custom_call_target="tpu_custom_call" | custom-call | tf_op jit(solution)/shard_map/pallas_call | solution.py:690
  506.2 1.4 shard_map.86

commit v4 on v3

--- a/solution.py
+++ b/solution.py
@@ -262,18 +262,21 @@
     across_from = far_targets(me, peers)
     held = across_from[near // 2 :]
 
-    def one(m, e, s, scale_of, hold=False):
-        for far in (True, False):
-            low, count = half(me < near, tiles, far)
-            for c in range(count):
-                at = pl.ds(pl.multiple_of((low + c) * LANES, LANES), LANES)
-                send[m, e, at, :] = (slots[s, :, at] / scale_of(low + c)).T.astype(send.dtype)
-            targets = [partner(k) for k in range(1, near)]
-            if far:
-                targets = across_from[: near // 2] if hold else across_from
-            for to in targets:
-                send_copy(m, to, e, 1).start()
+    def rescale(m, e, s, scale_of, low, count):
+        for c in range(count):
+            at = pl.ds(pl.multiple_of((low + c) * LANES, LANES), LANES)
+            send[m, e, at, :] = (slots[s, :, at] / scale_of(low + c)).T.astype(send.dtype)
+
+    def send_near(m, e):
+        for k in range(1, near):
+            send_copy(m, partner(k), e, 1).start()
         keep_copy(m, e, 1).start()
+
+    def one(m, e, s, scale_of):
+        rescale(m, e, s, scale_of, 0, tiles)
+        send_near(m, e)
+        for to in across_from:
+            send_copy(m, to, e, 1).start()
 
     def bulk(q, start, stop, first):
         m, _, _ = stream[q]
@@ -297,7 +300,15 @@
             seen_copy(e, k).wait_recv()
         opening[e, :tiles, :] = jnp.max(seen[e, :, :tiles, :], axis=0)
         _, s = arrived(q, i)
-        one(0, e, s, lambda c: opening[e, pl.ds(c, 1), :], hold)
+
+        def scale_of(c):
+            return opening[e, pl.ds(c, 1), :]
+
+        rescale(0, e, s, scale_of, *half(me < near, tiles, True))
+        for to in across_from[: near // 2] if hold else across_from:
+            send_copy(0, to, e, 1).start()
+        rescale(0, e, s, scale_of, *half(me < near, tiles, False))
+        send_near(0, e)
         fetch_start(bases[q] + i + SLOTS)
 
     depth = router.shape[0]
@@ -598,10 +609,11 @@
 
         @pl.when(lax.rem(lax.axis_index("owner"), len(LATER)) == turn)
         def _():
+            for i in range(later):
+                there = up.at[pl.ds(experts - later + i, 1)]
+                pltpu.make_async_copy(last.at[pl.ds(i, 1)], there, sem).start()
             there = up.at[pl.ds(experts - later, later)]
-            copy = pltpu.make_async_copy(last.at[pl.ds(0, later)], there, sem)
-            copy.start()
-            copy.wait()
+            pltpu.make_async_copy(last.at[pl.ds(0, later)], there, sem).wait()
 
 
 def fused(owners, peers, master_gate, master_up, router_weight, router_gain):

time: 508 us -> 508 us (level)
  no operation moved by 1% of the time
where the time goes in v4:
time: 508 us
  Pallas kernels  507 us (100%)
    pallas_call x1, Pallas kernels, fused(): pl.pallas_call(functools.partial(kernel, owners, peers), out_shape=(turne...  471 us
    pallas_call x1, Pallas kernels, fused(): pl.pallas_call(functools.partial(last_kernel, peers), out_shape=jax.Shape...  27.3 us

profile of v4, /device:TPU:15, one launch (start us, length us, event | category | flops | bytes accessed | tf_op | source)
XLA Modules:
  0.0 507.5 jit_solution(15212514781396372943)
XLA Ops:
  0.6 470.9 %shard_map.83 = (bf16[16,176,2048]{2,1,0:T(8,128)(2,1)S(1)}, bf16[16,176,2048]{2,1,0:T(8,128)(2,1)S(1)}, bf16[64,2048]{1,0:T(8,128)(2,1)S(1)}, f32[16,176]{1,0:T...) custom-call(f32[16,256,1408]{2,1,0:T(8,128)} %gate.1, f32[16,256,1408]{2,1,0:T(8,128)} %up.3, ...), custom_call_target="tpu_custom_call" | custom-call | tf_op jit(solution)/shard_map/pallas_call | solution.py:641
  471.5 7.3 %shard_map.84 = (bf16[16,176,2048]{2,1,0:T(8,128)(2,1)}, bf16[16,176,2048]{2,1,0:T(8,128)(2,1)}, bf16[64,2048]{1,0:T(8,128)(2,1)}, f32[16,176]{1,0:T(8,128)}, f3...) custom-call(bf16[16,176,2048]{2,1,0:T(8,128)(2,1)S(1)} %get-tuple-element.17.gate, ...), custom_call_target="tpu_custom_call" | custom-call | tf_op jit(solution)/shard_map/pallas_call | solution.py:693
  478.8 27.3 %shard_map.85.last = bf16[3,176,2048]{2,1,0:T(8,128)(2,1)S(1)} custom-call(f32[16,256,1408]{2,1,0:T(8,128)} %up.3, f32[11,8,128]{2,1,0:T(8,128)S(1)} %get-tuple-element.25.scales), custom_call_target="tpu_custom_call" | custom-call | tf_op jit(solution)/shard_map/pallas_call | solution.py:702
  506.2 1.4 shard_map.86
